TPU v7x, 32 devices: a whole 2x2x4 slice. The times are simulated.
32 devices in a mesh: row: 4 (over y, core), col: 8 (over z, x).
Axes of the slice: x: 2, y: 2, z: 4, core: 2. Of those that a mesh axis runs over, the one named last changes fastest.
Arguments:
- queries: bfloat16 [128, 128, 1024], P(('row', 'col')), may hold values from -6 to 6
- coarse_keys: bfloat16 [512, 1024], P('row'), may hold values from -6 to 6
- fine_keys: bfloat16 [4096, 1024], P('col'), may hold values from -6 to 6
- super_ids: int32 [128, 16], P(('row', 'col')), may hold values from 0 to 511, as said below
- picks: int32 [128, 64], P(('row', 'col')), may hold values from 0 to 127, as said below
Outputs:
- importance: float32 [128, 8, 512], P(('row', 'col'))
- selected: float32 [128, 512], P(('row', 'col'))
Inputs may be any that keep to these rules, and one draw needn't show every extreme that they name: `super_ids`: within each aligned run of 4 query blocks (the query blocks of one device), at most 16 of the ids lie in any one aligned range of 64 superblocks, and some range holds exactly 16; in some aligned group of 8 consecutive runs, one range holds exactly 16 ids of every run. Ids may repeat. `picks`: the numbers of a row are distinct; pick p names fine block p % 8 of superblock super_ids[b, p // 8]. Within each aligned run of 4 query blocks, at most 64 of the named fine blocks lie in any one aligned range of 64 superblocks, and some range holds exactly 64.
All inputs are finite; a program needn't handle non-finite values.
Results may differ from a plain program's by a relative error of at most 0.0003.
Values may be sent and summed in bfloat16 or wider, within the bound.
A program may use at most 64 MiB of HBM per device.

v0:
```python
import math

import jax
import jax.numpy as jnp
from jax import lax
from jax.sharding import PartitionSpec as P

H = 8
D = 128
SBLK = 8
PICK = 64


def pack_requests(owners, local_ids, ncols, capacity):
    marks = (owners[:, None] == jnp.arange(ncols, dtype=jnp.int32)[None, :]).astype(jnp.int32)
    earlier = jnp.cumsum(marks, axis=0) - marks
    slots = jnp.sum(earlier * marks, axis=1)
    places = owners * capacity + slots
    cells = jnp.arange(ncols * capacity, dtype=jnp.int32)
    matches = places[:, None] == cells[None, :]
    outgoing = jnp.sum(jnp.where(matches, local_ids[:, None] + 1, 0), axis=0) - 1
    return (outgoing.reshape(ncols, capacity), places)


def per_device(queries, coarse_keys, fine_keys, super_ids, picks):
    factor = 1.0 / math.sqrt(D)
    blocks, qtok, width = queries.shape
    supers = coarse_keys.shape[0] * lax.axis_size("row")
    ncols = lax.axis_size("col")
    qheads = queries.reshape(blocks, qtok, H, D)

    def block_scores(query_block, block_keys):
        keyed = block_keys.reshape(block_keys.shape[0], H, D)
        return (
            jnp.einsum("thd,nhd->htn", query_block, keyed, preferred_element_type=jnp.float32)
            * factor
        )

    start_max = jnp.full((blocks, H, qtok), -1e30, jnp.float32)
    start_totals = jnp.zeros((blocks, H, qtok), jnp.float32)
    gathered = lax.all_gather(coarse_keys, "row", axis=0, tiled=True)

    def stat_per_block(inputs):
        query_block, running_max, totals = inputs
        scores = block_scores(query_block, gathered)
        new_max = jnp.maximum(running_max, jnp.max(scores, axis=-1))
        totals = totals * jnp.exp(running_max - new_max) + jnp.sum(
            jnp.exp(scores - new_max[..., None]), axis=-1
        )
        return (new_max, totals)

    running_max, totals = lax.map(stat_per_block, (qheads, start_max, start_totals))

    def make_per_block(inputs):
        query_block, block_max, block_totals = inputs
        scores = block_scores(query_block, gathered)
        softened = jnp.exp(scores - block_max[..., None]) / block_totals[..., None]
        return jnp.sum(softened, axis=1) * (supers / qtok)

    portion = lax.map(make_per_block, (qheads, running_max, totals))
    sup_dev = fine_keys.shape[0] // SBLK
    parents = jnp.take_along_axis(super_ids, picks // SBLK, axis=1)
    capacity = blocks // 4 * PICK
    span = sup_dev * SBLK
    fine_ids = parents * SBLK + picks % SBLK
    owners = (fine_ids // span).reshape(-1)
    local_ids = (fine_ids % span).reshape(-1)
    outgoing, places = pack_requests(owners, local_ids, ncols, capacity)
    found = jnp.take(
        fine_keys,
        jnp.clip(
            lax.all_to_all(outgoing, "col", split_axis=0, concat_axis=0, tiled=True), 0, span - 1
        ),
        axis=0,
    )
    replies = lax.all_to_all(found, "col", split_axis=0, concat_axis=0, tiled=True)
    fetched = jnp.take(replies.reshape(ncols * capacity, width), places, axis=0)
    fetched = fetched.reshape(blocks, PICK, H, D)
    weights = jnp.take_along_axis(
        portion, jnp.broadcast_to(parents[:, None, :], (blocks, H, PICK)), axis=2
    )
    scores = (
        jnp.einsum("bthd,bjhd->bhtj", qheads, fetched, preferred_element_type=jnp.float32) * factor
    )
    softened = jax.nn.softmax(scores, axis=-1)
    selected = jnp.sum(softened, axis=2) * weights * (PICK / qtok)
    return (portion, selected.reshape(blocks, H * PICK))


def solution(mesh):
    return jax.shard_map(
        per_device,
        mesh=mesh,
        in_specs=(
            P(("row", "col"), None, None),
            P("row", None),
            P("col", None),
            P(("row", "col"), None),
            P(("row", "col"), None),
        ),
        out_specs=(P(("row", "col"), None, None), P(("row", "col"), None)),
        check_vma=False,
    )
```

profile of v0, /device:TPU:0, one launch (start us, length us, event | category | flops | bytes accessed | tf_op | source)
XLA Modules:
  0.0 85.9 jit_solution(12894194768072370491)
XLA Ops:
  7.2 0.8 bitcast_or_fusion
  8.1 2.3 %gather_fusion.2 = s32[256]{0:T(256)S(1)} fusion(s32[4,16]{1,0:T(4,128)} %param.12, s32[256]{0:T(256)S(1)} %reshape.247), kind=kCustom, calls=%fused_computation.2 | custom fusion | bytes 4096 | tf_op jit(solution)/shard_map/jit(take_along_axis)/gather | solution.py:62
  12.6 7.3 %all-to-all-start = ((s32[8,1,64]{2,1,0:T(1,128)}), s32[8,1,64]{2,1,0:T(1,128)S(1)}, u32[]{:S(2)}, u32[]{:S(2)}) async-start(s32[8,1,64]{2,1,0:T(1,128)} %sub.59), calls=%async_computation | async-start | bytes 8192 | tf_op jit(solution)/shard_map/all_to_all | solution.py:72
  19.9 0.7 all-gather.2.cloned.1.call-update
  21.6 1.0 %copy-done.2 = bf16[4,128,1024]{1,2,0:T(8,128)(2,1)} copy-done((bf16[4,128,1024]{1,2,0:T(8,128)(2,1)}, bf16[4,128,1024]{1,2,0:T(8,128)(2,1)S(1)}, u32[]{:S(2)}) %copy-start.2) | copy-done | bytes 1048600
  23.3 3.0 %all-to-all-done = s32[8,1,64]{2,1,0:T(1,128)S(1)} async-done(((s32[8,1,64]{2,1,0:T(1,128)}), s32[8,1,64]{2,1,0:T(1,128)S(1)}, u32[]{:S(2)}, u32[]{:S(2)}) %all-to-all-start) | async-done | bytes 2080 | tf_op jit(solution)/shard_map/all_to_all | solution.py:72
  26.4 2.1 %gather_fusion = bf16[512,1024]{1,0:T(8,128)(2,1)S(1)} fusion(bf16[512,1024]{1,0:T(8,128)(2,1)S(1)} %copy-done, s32[1024]{0:T(1024)S(1)} %pad_clamp_fusion.1), kind=kCustom, calls=%fused_computation | custom fusion | bytes 2099200 | tf_op jit(solution)/shard_map/jit(_take)/gather | solution.py:69
  28.5 1.2 %broadcast_select_fusion = bf16[8,64,1024]{2,1,0:T(8,128)(2,1)} fusion(bf16[8,64,1024]{2,1,0:T(8,128)(2,1)S(1)} %bitcast.99, pred[8,64]{1,0:T(8,128)(4,1)S(1)} %compare_and_fusion), kind=kLoop, calls=%fused_computation.36 | loop fusion | flops 524288 | bytes 2097664 | tf_op jit(solution)/shard_map/jit(_take)/select_n | solution.py:69
  29.7 3.6 %all-to-all-start.1 = ((bf16[8,64,1024]{2,1,0:T(8,128)(2,1)}), bf16[8,64,1024]{2,1,0:T(8,128)(2,1)S(1)}, u32[]{:S(2)}, u32[]{:S(2)}) async-start(bf16[8,64,1024]{2,1,0:T(8,128)(2,1)} %broadcast_select_fusion), calls=%async_computation.1 | async-start | bytes 2097152 | tf_op jit(solution)/shard_map/all_to_all | solution.py:76
  33.2 7.2 %all-gather.2.cloned.1.call-done = bf16[512,1024]{1,0:T(8,128)(2,1)} async-done(((bf16[128,1024]{1,0:T(8,128)(2,1)}), bf16[512,1024]{1,0:T(8,128)(2,1)}) %all-gather.2.cloned.1.call-update) | async-done | bytes 1048592 | tf_op jit(solution)/shard_map/all_gather | solution.py:41
  40.4 9.6 %while.22 = (s32[]{:T(128)}, f32[4,8,128]{2,1,0:T(8,128)S(1)}, f32[4,8,128]{2,1,0:T(8,128)S(1)}, bf16[4,128,8,128]{3,1,2,0:T(8,128)(2,1)S(1)}, bf16[512,1024]{1,0:T(8,128)(2,1)}, /*index=5*/s32[]{:T(128)}) while((s32[]{:T(128)}, f32[4,8,128]{2,1,0:T(8,128)S(1)}, f32[4,8,128]{2,1,0:T(8,128)S(1)}, bf16[4,128,8,128]{3,1,2,0:T(8,128)(2,1)S(1)}, ...), condition=%wide.region_3.4_spmd, body=%wide.region_0.3_spmd.sunk | while | flops 136842240 | bytes 5541965 | solution.py:52
  40.4 1.8 %multiply_reduce_fusion.2 = (f32[8,128]{1,0:T(8,128)S(1)}, f32[8,128,512]{2,1,0:T(8,128)S(1)}) fusion(bf16[4,128,8,128]{3,1,2,0:T(8,128)(2,1)S(1)} %get-tuple-element.227, s32[]{:T(128)} %get-tuple-element.218, bf16[512,1024]{1,0:T(8,128)(2,1)} %get-tuple-element.228), kind=kOutput, calls=%fused_computation.5.clone.1 | convolution fusion | flops 135265280 | bytes 3411972 | tf_op jit(solution)/shard_map/while/body/eval_jaxpr/thd,nhd->htn/dot_general | solution.py:35
  42.8 1.8 %multiply_reduce_fusion.2 = (f32[8,128]{1,0:T(8,128)S(1)}, f32[8,128,512]{2,1,0:T(8,128)S(1)}) fusion(bf16[4,128,8,128]{3,1,2,0:T(8,128)(2,1)S(1)} %get-tuple-element.227, s32[]{:T(128)} %get-tuple-element.218, bf16[512,1024]{1,0:T(8,128)(2,1)} %get-tuple-element.228), kind=kOutput, calls=%fused_computation.5.clone.1 | convolution fusion | flops 135265280 | bytes 3411972 | tf_op jit(solution)/shard_map/while/body/eval_jaxpr/thd,nhd->htn/dot_general | solution.py:35
  45.2 1.8 %multiply_reduce_fusion.2 = (f32[8,128]{1,0:T(8,128)S(1)}, f32[8,128,512]{2,1,0:T(8,128)S(1)}) fusion(bf16[4,128,8,128]{3,1,2,0:T(8,128)(2,1)S(1)} %get-tuple-element.227, s32[]{:T(128)} %get-tuple-element.218, bf16[512,1024]{1,0:T(8,128)(2,1)} %get-tuple-element.228), kind=kOutput, calls=%fused_computation.5.clone.1 | convolution fusion | flops 135265280 | bytes 3411972 | tf_op jit(solution)/shard_map/while/body/eval_jaxpr/thd,nhd->htn/dot_general | solution.py:35
  47.6 1.8 %multiply_reduce_fusion.2 = (f32[8,128]{1,0:T(8,128)S(1)}, f32[8,128,512]{2,1,0:T(8,128)S(1)}) fusion(bf16[4,128,8,128]{3,1,2,0:T(8,128)(2,1)S(1)} %get-tuple-element.227, s32[]{:T(128)} %get-tuple-element.218, bf16[512,1024]{1,0:T(8,128)(2,1)} %get-tuple-element.228), kind=kOutput, calls=%fused_computation.5.clone.1 | convolution fusion | flops 135265280 | bytes 3411972 | tf_op jit(solution)/shard_map/while/body/eval_jaxpr/thd,nhd->htn/dot_general | solution.py:35
  50.0 8.1 %while.23 = (s32[]{:T(128)}, f32[4,8,512]{2,1,0:T(8,128)S(1)}, bf16[4,128,8,128]{3,1,2,0:T(8,128)(2,1)S(1)}, bf16[512,1024]{1,0:T(8,128)(2,1)}, f32[4,8,128]{2,1...) while((s32[]{:T(128)}, f32[4,8,512]{2,1,0:T(8,128)S(1)}, bf16[4,128,8,128]{3,1,2,0:T(8,128)(2,1)S(1)}, ...), condition=%wide.region_6.7_spmd, body=%wide.region_4.6_spmd.sunk | while | flops 136314880 | bytes 1384537 | solution.py:60
  50.0 2.0 %fusion.49 = f32[8,512]{1,0:T(8,128)S(1)} fusion(f32[8,128]{1,0:T(8,128)S(1)} %get-tuple-element.210, f32[8,128]{1,0:T(8,128)S(1)} %get-tuple-element.211, bf16[4,128,8,128]{3,1,2,0:T(8,128)(2,1)S(1)} %get-tuple-element.246, s32[]{:T(128)} %get-tuple-element.237, bf16[512,1024]{1,0:T(8,128)(2,1)} %get-tuple-element.247), kind=kOutput, calls=%fused_computation.20.clone.1 | convolution fusion | flops 136310784 | bytes 1335300 | tf_op jit(solution)/shard_map/while/body/eval_jaxpr/thd,nhd->htn/dot_general | solution.py:35
  52.1 2.0 %fusion.49 = f32[8,512]{1,0:T(8,128)S(1)} fusion(f32[8,128]{1,0:T(8,128)S(1)} %get-tuple-element.210, f32[8,128]{1,0:T(8,128)S(1)} %get-tuple-element.211, bf16[4,128,8,128]{3,1,2,0:T(8,128)(2,1)S(1)} %get-tuple-element.246, s32[]{:T(128)} %get-tuple-element.237, bf16[512,1024]{1,0:T(8,128)(2,1)} %get-tuple-element.247), kind=kOutput, calls=%fused_computation.20.clone.1 | convolution fusion | flops 136310784 | bytes 1335300 | tf_op jit(solution)/shard_map/while/body/eval_jaxpr/thd,nhd->htn/dot_general | solution.py:35
  54.1 2.0 %fusion.49 = f32[8,512]{1,0:T(8,128)S(1)} fusion(f32[8,128]{1,0:T(8,128)S(1)} %get-tuple-element.210, f32[8,128]{1,0:T(8,128)S(1)} %get-tuple-element.211, bf16[4,128,8,128]{3,1,2,0:T(8,128)(2,1)S(1)} %get-tuple-element.246, s32[]{:T(128)} %get-tuple-element.237, bf16[512,1024]{1,0:T(8,128)(2,1)} %get-tuple-element.247), kind=kOutput, calls=%fused_computation.20.clone.1 | convolution fusion | flops 136310784 | bytes 1335300 | tf_op jit(solution)/shard_map/while/body/eval_jaxpr/thd,nhd->htn/dot_general | solution.py:35
  56.1 2.0 %fusion.49 = f32[8,512]{1,0:T(8,128)S(1)} fusion(f32[8,128]{1,0:T(8,128)S(1)} %get-tuple-element.210, f32[8,128]{1,0:T(8,128)S(1)} %get-tuple-element.211, bf16[4,128,8,128]{3,1,2,0:T(8,128)(2,1)S(1)} %get-tuple-element.246, s32[]{:T(128)} %get-tuple-element.237, bf16[512,1024]{1,0:T(8,128)(2,1)} %get-tuple-element.247), kind=kOutput, calls=%fused_computation.20.clone.1 | convolution fusion | flops 136310784 | bytes 1335300 | tf_op jit(solution)/shard_map/while/body/eval_jaxpr/thd,nhd->htn/dot_general | solution.py:35
  58.1 16.3 %gather_fusion.3 = f32[2048]{0:T(1024)S(1)} fusion(f32[4,8,512]{2,1,0:T(8,128)S(1)} %get-tuple-element.60, s32[2048]{0:T(1024)S(1)} %reshape.253), kind=kCustom, calls=%fused_computation.3 | custom fusion | bytes 40960 | tf_op jit(solution)/shard_map/jit(take_along_axis)/gather | solution.py:79
  74.5 2.0 %gather_fusion.1 = bf16[256,1024]{1,0:T(8,128)(2,1)} fusion(bf16[512,1024]{1,0:T(8,128)(2,1)S(1)} %bitcast.98, s32[1024]{0:T(1024)S(1)} %pad_clamp_fusion), kind=kCustom, calls=%fused_computation.1 | custom fusion | bytes 1049600 | tf_op jit(solution)/shard_map/jit(_take)/gather | solution.py:77
  76.5 1.1 %copy.34 = bf16[32,8,8,128]{3,2,1,0:T(8,128)(2,1)S(1)} copy(bf16[32,8,8,128]{3,1,2,0:T(8,128)(2,1)} %bitcast.102) | data formatting | bytes 1048576
  77.6 0.7 fusion.34
  (71 shorter events, 7.2 us)
Async XLA Ops:
  7.2 19.3 %copy-start = (bf16[512,1024]{1,0:T(8,128)(2,1)S(1)}, bf16[512,1024]{1,0:T(8,128)(2,1)}, u32[]{:S(2)}) copy-start(bf16[512,1024]{1,0:T(8,128)(2,1)} %param.11) | copy-start | bytes 3145732
  7.2 3.4 %copy-start.5 = (s32[4,64]{1,0:T(4,128)S(1)}, s32[4,64]{1,0:T(4,128)}, u32[]{:S(2)}) copy-start(s32[4,64]{1,0:T(4,128)} %param.13) | copy-start | bytes 3076
  7.2 13.7 %copy-start.4 = (bf16[4,128,1024]{2,1,0:T(8,128)(2,1)S(1)}, bf16[4,128,1024]{2,1,0:T(8,128)(2,1)}, u32[]{:S(2)}) copy-start(bf16[4,128,1024]{2,1,0:T(8,128)(2,1)} %param.9) | copy-start | bytes 3145732
  12.6 13.7 %all-to-all-start = ((s32[8,1,64]{2,1,0:T(1,128)}), s32[8,1,64]{2,1,0:T(1,128)S(1)}, u32[]{:S(2)}, u32[]{:S(2)}) async-start(s32[8,1,64]{2,1,0:T(1,128)} %sub.59), calls=%async_computation | async-start | bytes 8192 | tf_op jit(solution)/shard_map/all_to_all | solution.py:72
  19.9 20.5 %all-gather.2.cloned.1.call-start = ((), (), s32[]{:S(2)}) async-start(), calls=%async_computation.2 | async-start | bytes 1310720 | tf_op jit(solution)/shard_map/all_gather | solution.py:41
  21.6 1.0 %copy-start.2 = (bf16[4,128,1024]{1,2,0:T(8,128)(2,1)}, bf16[4,128,1024]{1,2,0:T(8,128)(2,1)S(1)}, u32[]{:S(2)}) copy-start(bf16[4,128,1024]{1,2,0:T(8,128)(2,1)S(1)} %copy.26) | copy-start | bytes 3145732
  29.7 44.8 %all-to-all-start.1 = ((bf16[8,64,1024]{2,1,0:T(8,128)(2,1)}), bf16[8,64,1024]{2,1,0:T(8,128)(2,1)S(1)}, u32[]{:S(2)}, u32[]{:S(2)}) async-start(bf16[8,64,1024]{2,1,0:T(8,128)(2,1)} %broadcast_select_fusion), calls=%async_computation.1 | async-start | bytes 2097152 | tf_op jit(solution)/shard_map/all_to_all | solution.py:76
  58.1 16.3 %copy-start.1 = (f32[4,8,512]{2,1,0:T(8,128)}, f32[4,8,512]{2,1,0:T(8,128)S(1)}, u32[]{:S(2)}) copy-start(f32[4,8,512]{2,1,0:T(8,128)S(1)} %get-tuple-element.60) | copy-start | bytes 196612
  74.5 3.1 %copy-start.3 = (bf16[4,128,1024]{1,2,0:T(8,128)(2,1)S(1)}, bf16[4,128,1024]{1,2,0:T(8,128)(2,1)}, u32[]{:S(2)}) copy-start(bf16[4,128,1024]{1,2,0:T(8,128)(2,1)} %copy-done.2) | copy-start | bytes 3145732
Sparse Core Ops, SparseCore 0:
  22.3 18.1 all-gather.1
where the time goes:
time: 86.5 us; the launch traced here: 85.9 us
  local copies, waits for them, and re-layouts  28.5 us (33%)
  matrix products  15.6 us (18%)
  between operations  14.3 us (17%)
  starting transfers between devices  10.9 us (13%)
  waiting for transfers between devices  10.9 us (13%)
  other arithmetic  5.45 us (6%)
    gather x3, local copies, waits for them, and re-layouts, per_device(): jnp.take_along_axis(portion, jnp.broadcast_to(parents[:, None, :], (block...  16.4 us
    dot_general x8, matrix products, block_scores(): jnp.einsum('thd,nhd->htn', query_block, keyed, preferred_element_type=jnp...  14.9 us
    all_to_all x1, starting transfers between devices, per_device(): lax.all_to_all(outgoing, 'col', split_axis=0, concat_axis=0, tiled=True)  7.28 us
    all_gather x1, waiting for transfers between devices, per_device(): gathered = lax.all_gather(coarse_keys, 'row', axis=0, tiled=True)  7.22 us
    all_to_all x1, starting transfers between devices, per_device(): lax.all_to_all(found, 'col', split_axis=0, concat_axis=0, tiled=True)  3.56 us
    all_to_all x1, waiting for transfers between devices, per_device(): lax.all_to_all(outgoing, 'col', split_axis=0, concat_axis=0, tiled=True)  3.04 us
    unnamed x14, local copies, waits for them, and re-layouts  2.8 us
    gather x3, local copies, waits for them, and re-layouts, per_device(): parents = jnp.take_along_axis(super_ids, picks // SBLK, axis=1)  2.49 us
  transfers between devices with their start and end apart: 3, of which 2 were waited for; matrix products, arithmetic and copies ran while one was open for 45% of the time, Pallas kernels for 0%

commit v1 on v0

v1 whole, which is shorter than its diff:
```python
import functools
import math

import jax
import jax.numpy as jnp
from jax import lax
from jax.experimental import pallas as pl
from jax.experimental.pallas import tpu as pltpu
from jax.sharding import PartitionSpec as P

H = 8
D = 128
SBLK = 8
PICK = 64
LANES = 128
GROUP = 4
MESH = pl.DeviceIdType.MESH


def pack_requests(owners, local_ids, ncols, capacity):
    count = owners.shape[0]
    order = jnp.arange(count, dtype=jnp.int32)
    earlier = (owners[:, None] == owners[None, :]) & (order[None, :] < order[:, None])
    slots = jnp.sum(earlier.astype(jnp.int32), axis=1)
    places = owners * capacity + slots
    cells = jnp.arange(ncols * capacity, dtype=jnp.int32)
    matches = places[:, None] == cells[None, :]
    outgoing = jnp.sum(jnp.where(matches, local_ids[:, None] + 1, 0), axis=0) - 1
    return (outgoing.reshape(ncols, capacity), places)


def kernel(
    nrows,
    ncols,
    capacity,
    request_ref,
    place_ref,
    parent_ref,
    query_hbm,
    coarse_hbm,
    fine_hbm,
    portion_ref,
    selected_ref,
    query,
    fine,
    coarse,
    asked,
    staged,
    replies,
    weights,
    local_sem,
    coarse_send,
    coarse_recv,
    ask_send,
    ask_recv,
    reply_send,
    reply_recv,
):
    row = lax.axis_index("row")
    col = lax.axis_index("col")
    blocks, qtok, width = query.shape
    supers = nrows * coarse.shape[1]
    span = fine.shape[0]
    scale = math.log2(math.e) / math.sqrt(D)

    fine_copy = pltpu.make_async_copy(fine_hbm, fine, local_sem.at[0])
    query_copy = pltpu.make_async_copy(query_hbm, query, local_sem.at[1])
    own_copy = pltpu.make_async_copy(coarse_hbm, coarse.at[row], local_sem.at[2])
    fine_copy.start()
    query_copy.start()
    own_copy.start()

    barrier = pltpu.get_barrier_semaphore()

    def greet_col(k, carry):
        peer = lax.rem(col + k, ncols)
        pl.semaphore_signal(barrier, inc=1, device_id=(row, peer), device_id_type=MESH)
        return carry

    def greet_row(k, carry):
        peer = lax.rem(row + k, nrows)
        pl.semaphore_signal(barrier, inc=1, device_id=(peer, col), device_id_type=MESH)
        return carry

    lax.fori_loop(1, ncols, greet_col, 0)
    lax.fori_loop(1, nrows, greet_row, 0)
    pl.semaphore_wait(barrier, ncols + nrows - 2)

    def ask_copy(k):
        peer = lax.rem(col + k, ncols)
        return pltpu.make_async_remote_copy(
            src_ref=request_ref.at[peer],
            dst_ref=asked.at[k],
            send_sem=ask_send.at[k],
            recv_sem=ask_recv.at[k],
            device_id=(row, peer),
            device_id_type=MESH,
        )

    def reply_copy(k):
        peer = lax.rem(col - k + ncols, ncols)
        return pltpu.make_async_remote_copy(
            src_ref=staged.at[k],
            dst_ref=replies.at[col],
            send_sem=reply_send.at[k],
            recv_sem=reply_recv.at[k],
            device_id=(row, peer),
            device_id_type=MESH,
        )

    def coarse_copy(k):
        peer = lax.rem(row + k, nrows)
        return pltpu.make_async_remote_copy(
            src_ref=coarse_hbm,
            dst_ref=coarse.at[row],
            send_sem=coarse_send.at[k],
            recv_sem=coarse_recv.at[k],
            device_id=(peer, col),
            device_id_type=MESH,
        )

    def each(start, stop, act):
        def body(k, carry):
            act(k)
            return carry

        lax.fori_loop(start, stop, body, 0)

    each(1, ncols, lambda k: ask_copy(k).start())
    each(1, nrows, lambda k: coarse_copy(k).start())

    fine_copy.wait()
    asked[0] = request_ref[col]
    row_iota = lax.broadcasted_iota(jnp.int32, (capacity, span), 1)

    def stage_group(g, carry):
        picked = []
        for i in range(GROUP):
            k = g * GROUP + i

            @pl.when(k > 0)
            def _():
                ask_copy(k).wait_recv()

            ids = jnp.transpose(asked[k])[:capacity, 0:1]
            picked.append((ids == row_iota).astype(jnp.float32).astype(jnp.bfloat16))
        found = jnp.dot(
            jnp.concatenate(picked, axis=0), fine[...], preferred_element_type=jnp.float32
        ).astype(jnp.bfloat16)
        for i in range(GROUP):
            staged[g * GROUP + i] = found[i * capacity : (i + 1) * capacity]
        for i in range(GROUP):
            k = g * GROUP + i

            @pl.when(k > 0)
            def _():
                reply_copy(k).start()

        return carry

    lax.fori_loop(0, ncols // GROUP, stage_group, 0)
    replies[col] = staged[0]

    query_copy.wait()
    own_copy.wait()
    each(1, nrows, lambda k: coarse_copy(k).wait_recv())

    super_iota = lax.broadcasted_iota(jnp.int32, (supers, LANES), 0)

    def coarse_block(b, carry):
        for h in range(H):
            cut = pl.ds(h * D, D)
            keys = coarse[:, :, cut].reshape(supers, D)
            scores = lax.dot_general(
                query[b, :, cut], keys, (((1,), (1,)), ((), ())), preferred_element_type=jnp.float32
            )
            top = jnp.max(scores, axis=1, keepdims=True)
            raised = jnp.exp2((scores - top) * scale)
            share = 1.0 / jnp.sum(raised, axis=1, keepdims=True)
            portion_ref[b, h : h + 1, :] = jnp.sum(raised * share, axis=0, keepdims=True) * (
                supers / qtok
            )
        chosen = (parent_ref[b] == super_iota).astype(jnp.float32)
        weights[b] = jnp.dot(
            portion_ref[b],
            chosen,
            preferred_element_type=jnp.float32,
            precision=lax.Precision.HIGHEST,
        )
        return carry

    lax.fori_loop(0, blocks, coarse_block, 0)

    each(1, ncols, lambda k: reply_copy(k).wait_recv())
    places = jnp.transpose(place_ref[...])
    cell_iota = lax.broadcasted_iota(jnp.int32, (PICK, ncols * capacity), 1)
    sorter = jnp.concatenate(
        [
            (places[:PICK, b : b + 1] == cell_iota).astype(jnp.float32).astype(jnp.bfloat16)
            for b in range(blocks)
        ],
        axis=0,
    )
    fetched = jnp.dot(
        sorter,
        replies[...].reshape(ncols * capacity, width),
        preferred_element_type=jnp.float32,
    ).astype(jnp.bfloat16)
    for b in range(blocks):
        sums = []
        for h in range(H):
            keys = fetched[b * PICK : (b + 1) * PICK, h * D : (h + 1) * D]
            scores = lax.dot_general(
                query[b, :, h * D : (h + 1) * D],
                keys,
                (((1,), (1,)), ((), ())),
                preferred_element_type=jnp.float32,
            )
            top = jnp.max(scores, axis=1, keepdims=True)
            raised = jnp.exp2((scores - top) * scale)
            share = 1.0 / jnp.sum(raised, axis=1, keepdims=True)
            sums.append(jnp.sum(raised * share, axis=0, keepdims=True))
        selected_ref[b] = (
            jnp.concatenate(sums, axis=0) * weights[b, :, :PICK] * (PICK / qtok)
        )

    each(1, ncols, lambda k: ask_copy(k).wait_send())
    each(1, ncols, lambda k: reply_copy(k).wait_send())
    each(1, nrows, lambda k: coarse_copy(k).wait_send())


def per_device(queries, coarse_keys, fine_keys, super_ids, picks):
    blocks, qtok, width = queries.shape
    nrows = lax.axis_size("row")
    ncols = lax.axis_size("col")
    shard = coarse_keys.shape[0]
    supers = shard * nrows
    span = fine_keys.shape[0]
    capacity = blocks // 4 * PICK
    candidate = picks // SBLK
    which = jnp.arange(super_ids.shape[1], dtype=jnp.int32)
    parents = jnp.sum(
        jnp.where(candidate[:, :, None] == which, super_ids[:, None, :], 0), axis=2
    )
    fine_ids = parents * SBLK + picks % SBLK
    owners = (fine_ids // span).reshape(-1)
    local_ids = (fine_ids % span).reshape(-1)
    outgoing, places = pack_requests(owners, local_ids, ncols, capacity)
    requests = jnp.broadcast_to(
        jnp.pad(outgoing, ((0, 0), (0, LANES - capacity)))[:, None, :], (ncols, 8, LANES)
    )
    placed = jnp.pad(places.reshape(blocks, PICK), ((0, 8 - blocks), (0, LANES - PICK)))
    parented = jnp.pad(parents, ((0, 0), (0, LANES - PICK)))[:, None, :]
    vmem = pl.BlockSpec(memory_space=pltpu.VMEM)
    anywhere = pl.BlockSpec(memory_space=pl.ANY)
    portion, selected = pl.pallas_call(
        functools.partial(kernel, nrows, ncols, capacity),
        out_shape=(
            jax.ShapeDtypeStruct((blocks, H, supers), jnp.float32),
            jax.ShapeDtypeStruct((blocks, H, PICK), jnp.float32),
        ),
        in_specs=[vmem] * 3 + [anywhere] * 3,
        out_specs=(vmem, vmem),
        scratch_shapes=[
            pltpu.VMEM((blocks, qtok, width), jnp.bfloat16),
            pltpu.VMEM((span, width), jnp.bfloat16),
            pltpu.VMEM((nrows, shard, width), jnp.bfloat16),
            pltpu.VMEM((ncols, 8, LANES), jnp.int32),
            pltpu.VMEM((ncols, capacity, width), jnp.bfloat16),
            pltpu.VMEM((ncols, capacity, width), jnp.bfloat16),
            pltpu.VMEM((blocks, H, LANES), jnp.float32),
            pltpu.SemaphoreType.DMA((3,)),
            pltpu.SemaphoreType.DMA((nrows,)),
            pltpu.SemaphoreType.DMA((nrows,)),
            pltpu.SemaphoreType.DMA((ncols,)),
            pltpu.SemaphoreType.DMA((ncols,)),
            pltpu.SemaphoreType.DMA((ncols,)),
            pltpu.SemaphoreType.DMA((ncols,)),
        ],
        compiler_params=pltpu.CompilerParams(
            collective_id=0, has_side_effects=True, vmem_limit_bytes=50 * 1024 * 1024
        ),
    )(requests, placed, parented, queries, coarse_keys, fine_keys)
    return (portion, selected.reshape(blocks, H * PICK))


def solution(mesh):
    return jax.shard_map(
        per_device,
        mesh=mesh,
        in_specs=(
            P(("row", "col"), None, None),
            P("row", None),
            P("col", None),
            P(("row", "col"), None),
            P(("row", "col"), None),
        ),
        out_specs=(P(("row", "col"), None, None), P(("row", "col"), None)),
        check_vma=False,
    )
```

time: 86.5 us -> 44 us (0.51)
  Pallas kernels: 0 us -> 36.2 us
  local copies, waits for them, and re-layouts: 28.5 us -> 5.72 us
  matrix products: 15.6 us -> 0 us
  between operations: 14.3 us -> 0.69 us
  starting transfers between devices: 10.9 us -> 0 us
  waiting for transfers between devices: 10.9 us -> 0 us
  other arithmetic: 5.45 us -> 1.16 us
    pallas_call x0 -> x1, Pallas kernels: none -> 36.2 us  [per_device(): pl.pallas_call(functools.partial(kernel, nrows, ncols, capacity), out_sha...]
    gather x8 -> x0, local copies, waits for them, and re-layouts: 22.9 us -> none  [the longest x3 16.4 us: per_device(): jnp.take_along_axis(portion, jnp.broadcast_to(parents[:, None, :], (block...]
    dot_general x8 -> x0, matrix products: 14.9 us -> none  [block_scores(): jnp.einsum('thd,nhd->htn', query_block, keyed, preferred_element_type=jnp...]
    all_to_all x2 -> x0, starting transfers between devices: 10.8 us -> none  [the longest x1 7.28 us: per_device(): lax.all_to_all(outgoing, 'col', split_axis=0, concat_axis=0, tiled=True)]
    all_gather x1 -> x0, waiting for transfers between devices: 7.22 us -> none  [per_device(): gathered = lax.all_gather(coarse_keys, 'row', axis=0, tiled=True)]
    all_to_all x2 -> x0, waiting for transfers between devices: 3.04 us -> none  [the longest x1 3.04 us: per_device(): lax.all_to_all(outgoing, 'col', split_axis=0, concat_axis=0, tiled=True)]
    reduce_sum x5 -> x2, other arithmetic: 2.45 us -> 0.27 us  [the longest x1 0.18 us: pack_requests(): slots = jnp.sum(earlier.astype(jnp.int32), axis=1)]
    unnamed x14 -> x11, local copies, waits for them, and re-layouts: 2.8 us -> 4.69 us
  transfers between devices with their start and end apart: 3 -> 0, of which waited for: 2 -> 0; matrix products, arithmetic and copies ran while one was open for 45% -> 0% of each run, Pallas kernels for 0% -> 0%
where the time goes in v1:
time: 44 us; the launch traced here: 43.7 us
  Pallas kernels  36.2 us (82%)
  local copies, waits for them, and re-layouts  5.72 us (13%)
  other arithmetic  1.16 us (3%)
  between operations  0.69 us (2%)
    pallas_call x1, Pallas kernels, per_device(): pl.pallas_call(functools.partial(kernel, nrows, ncols, capacity), out_sha...  36.2 us
    unnamed x11, local copies, waits for them, and re-layouts  4.69 us

profile of v1, /device:TPU:0, one launch (start us, length us, event | category | flops | bytes accessed | tf_op | source)
XLA Modules:
  0.0 43.7 jit_solution(9614103292152015559)
XLA Ops:
  0.6 0.0 copy-start.4
  0.6 0.7 %add_select_fusion.3 = s32[4,64]{1,0:T(4,128)S(1)} fusion(s32[4,64]{1,0:T(4,128)} %param.9), kind=kLoop, calls=%fused_computation.13 | loop fusion | flops 3840 | bytes 2048 | tf_op jit(solution)/shard_map/jit(floor_divide)/jit(_where)/select_n | solution.py:240
  1.3 0.0 copy-done.4
  1.3 0.1 select_reduce_fusion.1
  1.4 0.0 copy-start.3
  1.5 0.7 %copy-done.3 = s32[4,64]{1,0:T(4,128)S(1)} copy-done((s32[4,64]{1,0:T(4,128)S(1)}, s32[4,64]{1,0:T(4,128)}, u32[]{:S(2)}) %copy-start.3) | copy-done | bytes 1048
  2.1 0.1 reshape.38
  2.2 0.2 convert_reduce_fusion
  2.4 0.1 reduce_sum.32
  2.5 0.1 add.51
  2.6 0.2 select_reduce_fusion
  2.8 0.1 sub.19
  2.9 0.0 copy-start
  2.9 1.2 %copy-done = bf16[4,128,1024]{2,1,0:T(8,128)(2,1)S(1)} copy-done((bf16[4,128,1024]{2,1,0:T(8,128)(2,1)S(1)}, bf16[4,128,1024]{2,1,0:T(8,128)(2,1)}, u32[]{:S(2)}) %copy-start) | copy-done | bytes 1048600
  4.1 0.0 copy-start.1
  4.1 1.2 %copy-done.1 = bf16[512,1024]{1,0:T(8,128)(2,1)S(1)} copy-done((bf16[512,1024]{1,0:T(8,128)(2,1)S(1)}, bf16[512,1024]{1,0:T(8,128)(2,1)}, u32[]{:S(2)}) %copy-start.1) | copy-done | bytes 1048600
  5.3 0.0 copy-start.2
  5.3 0.9 %copy-done.2 = bf16[128,1024]{1,0:T(8,128)(2,1)S(1)} copy-done((bf16[128,1024]{1,0:T(8,128)(2,1)S(1)}, bf16[128,1024]{1,0:T(8,128)(2,1)}, u32[]{:S(2)}) %copy-start.2) | copy-done | bytes 262168
  6.3 36.2 %shard_map.68 = (f32[4,8,512]{2,1,0:T(8,128)S(1)}, f32[4,8,64]{2,1,0:T(8,128)S(1)}) custom-call(s32[8,8,128]{2,1,0:T(8,128)S(1)} %broadcast_in_dim.44.request_ref, s32[8,128]{1,0:T(8,128)S(1)} %pad.13.place_ref, s32[4,1,128]{2,1,0:T(1,128)S(1)} %bitcast.1, bf16[4,128,1024]{2,1,0:T(8,128)(2,1)S(1)} %copy-done, bf16[128,1024]{1,0:T(8,128)(2,1)S(1)} %copy-done.2, ...), custom_call_target="tpu_custom_call" | custom-call | tf_op jit(solution)/shard_map/pallas_call | solution.py:256
  42.4 0.7 %reshape.39 = f32[4,512]{1,0:T(4,128)} reshape(f32[4,8,64]{2,1,0:T(8,128)S(1)} %get-tuple-element.5) | data formatting | bytes 16384 | tf_op jit(solution)/shard_map/reshape | solution.py:284
  43.1 0.6 %copy.8 = f32[4,8,512]{2,1,0:T(8,128)} copy(f32[4,8,512]{2,1,0:T(8,128)S(1)} %get-tuple-element.12) | data formatting | bytes 131072
  (8 shorter events, 0.1 us)
Async XLA Ops:
  0.6 0.7 %copy-start.4 = (s32[4,16]{1,0:T(4,128)S(1)}, s32[4,16]{1,0:T(4,128)}, u32[]{:S(2)}) copy-start(s32[4,16]{1,0:T(4,128)} %param.8) | copy-start | bytes 772
  1.4 0.7 %copy-start.3 = (s32[4,64]{1,0:T(4,128)S(1)}, s32[4,64]{1,0:T(4,128)}, u32[]{:S(2)}) copy-start(s32[4,64]{1,0:T(4,128)} %param.9) | copy-start | bytes 3076
  2.9 1.2 %copy-start = (bf16[4,128,1024]{2,1,0:T(8,128)(2,1)S(1)}, bf16[4,128,1024]{2,1,0:T(8,128)(2,1)}, u32[]{:S(2)}) copy-start(bf16[4,128,1024]{2,1,0:T(8,128)(2,1)} %query_hbm.1) | copy-start | bytes 3145732
  4.1 1.2 %copy-start.1 = (bf16[512,1024]{1,0:T(8,128)(2,1)S(1)}, bf16[512,1024]{1,0:T(8,128)(2,1)}, u32[]{:S(2)}) copy-start(bf16[512,1024]{1,0:T(8,128)(2,1)} %fine_hbm.1) | copy-start | bytes 3145732
  5.3 0.9 %copy-start.2 = (bf16[128,1024]{1,0:T(8,128)(2,1)S(1)}, bf16[128,1024]{1,0:T(8,128)(2,1)}, u32[]{:S(2)}) copy-start(bf16[128,1024]{1,0:T(8,128)(2,1)} %coarse_hbm.1) | copy-start | bytes 786436

commit v2 on v1

v2 whole, which is shorter than its diff:
```python
import functools
import math

import jax
import jax.numpy as jnp
from jax import lax
from jax.experimental import pallas as pl
from jax.experimental.pallas import tpu as pltpu
from jax.sharding import PartitionSpec as P

H = 8
D = 128
SBLK = 8
PICK = 64
LANES = 128
GROUP = 4
MESH = pl.DeviceIdType.MESH


def pack_requests(owners, local_ids, ncols, capacity):
    count = owners.shape[0]
    order = jnp.arange(count, dtype=jnp.int32)
    earlier = (owners[:, None] == owners[None, :]) & (order[None, :] < order[:, None])
    slots = jnp.sum(earlier.astype(jnp.int32), axis=1)
    places = owners * capacity + slots
    cells = jnp.arange(ncols * capacity, dtype=jnp.int32)
    matches = places[:, None] == cells[None, :]
    outgoing = jnp.sum(jnp.where(matches, local_ids[:, None] + 1, 0), axis=0) - 1
    return (outgoing.reshape(ncols, capacity), places)


def kernel(
    nrows,
    ncols,
    capacity,
    request_ref,
    place_ref,
    parent_ref,
    query_hbm,
    coarse_hbm,
    fine_hbm,
    portion_ref,
    selected_ref,
    query,
    fine,
    coarse,
    across,
    asked,
    near_staged,
    far_staged,
    near,
    far,
    weights,
    local_sem,
    across_sem,
    coarse_send,
    coarse_recv,
    ask_send,
    ask_recv,
    near_send,
    near_recv,
    far_send,
    far_recv,
):
    row = lax.axis_index("row")
    col = lax.axis_index("col")
    half = ncols // 2
    team = nrows * half
    local = lax.rem(col, half)
    base = col - local
    me = row * half + local
    blocks, qtok, width = query.shape
    part = width // nrows
    supers = nrows * coarse.shape[1]
    span = fine.shape[0]
    scale = math.log2(math.e) / math.sqrt(D)

    fine_copy = pltpu.make_async_copy(fine_hbm, fine, local_sem.at[0])
    query_copy = pltpu.make_async_copy(query_hbm, query, local_sem.at[1])
    own_copy = pltpu.make_async_copy(coarse_hbm, coarse.at[row], local_sem.at[2])
    fine_copy.start()
    own_copy.start()
    query_copy.start()

    def each(start, stop, act):
        def body(k, carry):
            act(k)
            return carry

        lax.fori_loop(start, stop, body, 0)

    def ahead(k):
        peer = lax.rem(me + k, team)
        return (peer // half, base + lax.rem(peer, half))

    def behind(k):
        peer = lax.rem(me - k + team, team)
        return (peer // half, base + lax.rem(peer, half))

    opposite = (row, lax.rem(col + half, ncols))
    barrier = pltpu.get_barrier_semaphore()
    pl.semaphore_signal(barrier, inc=1, device_id=opposite, device_id_type=MESH)
    each(
        1,
        team,
        lambda k: pl.semaphore_signal(barrier, inc=1, device_id=ahead(k), device_id_type=MESH),
    )
    pl.semaphore_wait(barrier, team)

    def ask_copy(k):
        target = ahead(k)
        return pltpu.make_async_remote_copy(
            src_ref=request_ref.at[target[1] - base],
            dst_ref=asked.at[k],
            send_sem=ask_send.at[k],
            recv_sem=ask_recv.at[k],
            device_id=target,
            device_id_type=MESH,
        )

    across_copy = pltpu.make_async_remote_copy(
        src_ref=fine_hbm.at[:, pl.ds(pl.multiple_of(row * part, part), part)],
        dst_ref=across,
        send_sem=across_sem.at[0],
        recv_sem=across_sem.at[1],
        device_id=opposite,
        device_id_type=MESH,
    )

    def near_copy(k):
        return pltpu.make_async_remote_copy(
            src_ref=near_staged.at[k],
            dst_ref=near.at[local],
            send_sem=near_send.at[k],
            recv_sem=near_recv.at[k],
            device_id=(row, base + lax.rem(local - k + half, half)),
            device_id_type=MESH,
        )

    def far_copy(k):
        return pltpu.make_async_remote_copy(
            src_ref=far_staged.at[k],
            dst_ref=far.at[row, local],
            send_sem=far_send.at[k],
            recv_sem=far_recv.at[k],
            device_id=behind(k),
            device_id_type=MESH,
        )

    def coarse_copy(k):
        return pltpu.make_async_remote_copy(
            src_ref=coarse_hbm,
            dst_ref=coarse.at[row],
            send_sem=coarse_send.at[k],
            recv_sem=coarse_recv.at[k],
            device_id=(lax.rem(row + k, nrows), col),
            device_id_type=MESH,
        )

    each(1, team, lambda k: ask_copy(k).start())
    across_copy.start()
    each(1, nrows, lambda k: coarse_copy(k).start())

    asked[0] = request_ref[local]
    row_iota = lax.broadcasted_iota(jnp.int32, (capacity, span), 1)
    fine_copy.wait()
    each(1, team, lambda k: ask_copy(k).wait_recv())

    def one_hot(k, offset):
        ids = jnp.transpose(asked[k])[offset : offset + capacity, 0:1]
        return (ids == row_iota).astype(jnp.float32).astype(jnp.bfloat16)

    def near_group(g, carry):
        picked = []
        for i in range(GROUP):
            other = lax.rem(local - (g * GROUP + i) + half, half)
            picked.append(one_hot(lax.rem(local - other + team, team), 0))
        found = jnp.dot(
            jnp.concatenate(picked, axis=0), fine[...], preferred_element_type=jnp.float32
        ).astype(jnp.bfloat16)
        for i in range(GROUP):
            near_staged[g * GROUP + i] = found[i * capacity : (i + 1) * capacity]
        for i in range(GROUP):
            k = g * GROUP + i

            @pl.when(k > 0)
            def _():
                near_copy(k).start()

        return carry

    lax.fori_loop(0, half // GROUP, near_group, 0)
    near[local] = near_staged[0]
    across_copy.wait_recv()

    def far_group(g, carry):
        picked = [one_hot(g * GROUP + i, capacity) for i in range(GROUP)]
        found = jnp.dot(
            jnp.concatenate(picked, axis=0), across[...], preferred_element_type=jnp.float32
        ).astype(jnp.bfloat16)
        for i in range(GROUP):
            far_staged[g * GROUP + i] = found[i * capacity : (i + 1) * capacity]
        for i in range(GROUP):
            k = g * GROUP + i

            @pl.when(k > 0)
            def _():
                far_copy(k).start()

        return carry

    lax.fori_loop(0, team // GROUP, far_group, 0)
    far[row, local] = far_staged[0]

    query_copy.wait()
    own_copy.wait()
    each(1, nrows, lambda k: coarse_copy(k).wait_recv())

    super_iota = lax.broadcasted_iota(jnp.int32, (supers, LANES), 0)

    def coarse_block(b, carry):
        for h in range(H):
            cut = pl.ds(h * D, D)
            keys = coarse[:, :, cut].reshape(supers, D)
            scores = lax.dot_general(
                query[b, :, cut], keys, (((1,), (1,)), ((), ())), preferred_element_type=jnp.float32
            )
            top = jnp.max(scores, axis=1, keepdims=True)
            raised = jnp.exp2((scores - top) * scale)
            share = 1.0 / jnp.sum(raised, axis=1, keepdims=True)
            portion_ref[b, h : h + 1, :] = jnp.sum(raised * share, axis=0, keepdims=True) * (
                supers / qtok
            )
        chosen = (parent_ref[b] == super_iota).astype(jnp.float32)
        weights[b] = jnp.dot(
            portion_ref[b],
            chosen,
            preferred_element_type=jnp.float32,
            precision=lax.Precision.HIGHEST,
        )
        return carry

    lax.fori_loop(0, blocks, coarse_block, 0)

    places = jnp.transpose(place_ref[...])
    cell_iota = lax.broadcasted_iota(jnp.int32, (PICK, ncols * capacity), 1)
    sorter = jnp.concatenate(
        [
            (places[:PICK, b : b + 1] == cell_iota).astype(jnp.float32).astype(jnp.bfloat16)
            for b in range(blocks)
        ],
        axis=0,
    )
    cells = half * capacity
    each(1, half, lambda k: near_copy(k).wait_recv())
    each(1, team, lambda k: far_copy(k).wait_recv())
    sums = [[] for _ in range(blocks)]
    for q in range(nrows):
        rows = jnp.dot(
            sorter[:, :cells],
            near[:, :, q * part : (q + 1) * part].reshape(cells, part),
            preferred_element_type=jnp.float32,
        ) + jnp.dot(
            sorter[:, cells:],
            far[q].reshape(cells, part),
            preferred_element_type=jnp.float32,
        )
        rows = rows.astype(jnp.bfloat16)
        for b in range(blocks):
            for i in range(part // D):
                h = q * (part // D) + i
                scores = lax.dot_general(
                    query[b, :, h * D : (h + 1) * D],
                    rows[b * PICK : (b + 1) * PICK, i * D : (i + 1) * D],
                    (((1,), (1,)), ((), ())),
                    preferred_element_type=jnp.float32,
                )
                top = jnp.max(scores, axis=1, keepdims=True)
                raised = jnp.exp2((scores - top) * scale)
                share = 1.0 / jnp.sum(raised, axis=1, keepdims=True)
                sums[b].append(jnp.sum(raised * share, axis=0, keepdims=True))
    for b in range(blocks):
        selected_ref[b] = (
            jnp.concatenate(sums[b], axis=0) * weights[b, :, :PICK] * (PICK / qtok)
        )

    across_copy.wait_send()
    each(1, team, lambda k: ask_copy(k).wait_send())
    each(1, half, lambda k: near_copy(k).wait_send())
    each(1, team, lambda k: far_copy(k).wait_send())
    each(1, nrows, lambda k: coarse_copy(k).wait_send())


def per_device(queries, coarse_keys, fine_keys, super_ids, picks):
    blocks, qtok, width = queries.shape
    nrows = lax.axis_size("row")
    ncols = lax.axis_size("col")
    half = ncols // 2
    team = nrows * half
    shard = coarse_keys.shape[0]
    supers = shard * nrows
    span = fine_keys.shape[0]
    part = width // nrows
    capacity = blocks // 4 * PICK
    candidate = picks // SBLK
    which = jnp.arange(super_ids.shape[1], dtype=jnp.int32)
    parents = jnp.sum(
        jnp.where(candidate[:, :, None] == which, super_ids[:, None, :], 0), axis=2
    )
    fine_ids = parents * SBLK + picks % SBLK
    base = lax.axis_index("col") // half * half
    owners = ((fine_ids // span - base + ncols) % ncols).reshape(-1)
    local_ids = (fine_ids % span).reshape(-1)
    outgoing, places = pack_requests(owners, local_ids, ncols, capacity)
    outgoing = jnp.concatenate([outgoing[:half], outgoing[half:]], axis=1)
    requests = jnp.broadcast_to(outgoing[:, None, :], (half, 8, 2 * capacity))
    placed = jnp.pad(places.reshape(blocks, PICK), ((0, 8 - blocks), (0, LANES - PICK)))
    parented = jnp.pad(parents, ((0, 0), (0, LANES - PICK)))[:, None, :]
    vmem = pl.BlockSpec(memory_space=pltpu.VMEM)
    anywhere = pl.BlockSpec(memory_space=pl.ANY)
    dma = pltpu.SemaphoreType.DMA
    portion, selected = pl.pallas_call(
        functools.partial(kernel, nrows, ncols, capacity),
        out_shape=(
            jax.ShapeDtypeStruct((blocks, H, supers), jnp.float32),
            jax.ShapeDtypeStruct((blocks, H, PICK), jnp.float32),
        ),
        in_specs=[vmem] * 3 + [anywhere] * 3,
        out_specs=(vmem, vmem),
        scratch_shapes=[
            pltpu.VMEM((blocks, qtok, width), jnp.bfloat16),
            pltpu.VMEM((span, width), jnp.bfloat16),
            pltpu.VMEM((nrows, shard, width), jnp.bfloat16),
            pltpu.VMEM((span, part), jnp.bfloat16),
            pltpu.VMEM((team, 8, 2 * capacity), jnp.int32),
            pltpu.VMEM((half, capacity, width), jnp.bfloat16),
            pltpu.VMEM((team, capacity, part), jnp.bfloat16),
            pltpu.VMEM((half, capacity, width), jnp.bfloat16),
            pltpu.VMEM((nrows, half, capacity, part), jnp.bfloat16),
            pltpu.VMEM((blocks, H, LANES), jnp.float32),
            dma((3,)),
            dma((2,)),
            dma((nrows,)),
            dma((nrows,)),
            dma((team,)),
            dma((team,)),
            dma((half,)),
            dma((half,)),
            dma((team,)),
            dma((team,)),
        ],
        compiler_params=pltpu.CompilerParams(
            collective_id=0, has_side_effects=True, vmem_limit_bytes=50 * 1024 * 1024
        ),
    )(requests, placed, parented, queries, coarse_keys, fine_keys)
    return (portion, selected.reshape(blocks, H * PICK))


def solution(mesh):
    return jax.shard_map(
        per_device,
        mesh=mesh,
        in_specs=(
            P(("row", "col"), None, None),
            P("row", None),
            P("col", None),
            P(("row", "col"), None),
            P(("row", "col"), None),
        ),
        out_specs=(P(("row", "col"), None, None), P(("row", "col"), None)),
        check_vma=False,
    )
```

time: 44 us -> 40.4 us (0.918)
  Pallas kernels: 36.2 us -> 32.4 us
  local copies, waits for them, and re-layouts: 5.72 us -> 6.47 us
  other arithmetic: 1.16 us -> 0.56 us
    pallas_call x1, Pallas kernels: 36.2 us -> 32.4 us  [per_device(): pl.pallas_call(functools.partial(kernel, nrows, ncols, capacity), out_sha...]
    select_n x1, other arithmetic: 0.7 us -> 0.01 us  [per_device(): candidate = picks // SBLK]
    unnamed x11, local copies, waits for them, and re-layouts: 4.69 us -> 5.37 us
where the time goes in v2:
time: 40.4 us; the launch traced here: 40.1 us
  Pallas kernels  32.4 us (80%)
  local copies, waits for them, and re-layouts  6.47 us (16%)
  between operations  0.69 us (2%)
  other arithmetic  0.56 us (1%)
    pallas_call x1, Pallas kernels, per_device(): pl.pallas_call(functools.partial(kernel, nrows, ncols, capacity), out_sha...  32.4 us
    unnamed x11, local copies, waits for them, and re-layouts  5.37 us

profile of v2, /device:TPU:0, one launch (start us, length us, event | category | flops | bytes accessed | tf_op | source)
XLA Modules:
  0.0 40.1 jit_solution(3451698581683177620)
XLA Ops:
  0.6 0.0 copy-start.3
  0.7 0.7 %copy-done.3 = s32[4,64]{1,0:T(4,128)S(1)} copy-done((s32[4,64]{1,0:T(4,128)S(1)}, s32[4,64]{1,0:T(4,128)}, u32[]{:S(2)}) %copy-start.3) | copy-done | bytes 1048
  1.3 0.0 copy-start.4
  1.3 0.7 %copy-done.4 = s32[4,16]{1,0:T(4,128)S(1)} copy-done((s32[4,16]{1,0:T(4,128)S(1)}, s32[4,16]{1,0:T(4,128)}, u32[]{:S(2)}) %copy-start.4) | copy-done | bytes 280
  2.0 0.1 select_reduce_fusion.1
  2.1 0.1 reshape.45
  2.2 0.2 convert_reduce_fusion
  2.4 0.1 reduce_sum.32
  2.5 0.1 add.60
  2.6 0.2 select_reduce_fusion
  2.8 0.1 slice.17
  2.8 0.1 slice.19
  2.9 0.1 pad_add_fusion
  3.0 0.0 copy-start
  3.0 1.2 %copy-done = bf16[4,128,1024]{2,1,0:T(8,128)(2,1)S(1)} copy-done((bf16[4,128,1024]{2,1,0:T(8,128)(2,1)S(1)}, bf16[4,128,1024]{2,1,0:T(8,128)(2,1)}, u32[]{:S(2)}) %copy-start) | copy-done | bytes 1048600
  4.2 0.0 copy-start.1
  4.2 1.2 %copy-done.1 = bf16[512,1024]{1,0:T(8,128)(2,1)S(1)} copy-done((bf16[512,1024]{1,0:T(8,128)(2,1)S(1)}, bf16[512,1024]{1,0:T(8,128)(2,1)}, u32[]{:S(2)}) %copy-start.1) | copy-done | bytes 1048600
  5.5 0.0 copy-start.2
  5.5 0.9 %copy-done.2 = bf16[128,1024]{1,0:T(8,128)(2,1)S(1)} copy-done((bf16[128,1024]{1,0:T(8,128)(2,1)S(1)}, bf16[128,1024]{1,0:T(8,128)(2,1)}, u32[]{:S(2)}) %copy-start.2) | copy-done | bytes 262168
  6.4 32.4 %shard_map.68 = (f32[4,8,512]{2,1,0:T(8,128)S(1)}, f32[4,8,64]{2,1,0:T(8,128)S(1)}) custom-call(s32[4,8,128]{2,1,0:T(8,128)S(1)} %broadcast_in_dim.44.request_ref, s32[8,128]{1,0:T(8,128)S(1)} %pad.8.place_ref, s32[4,1,128]{2,1,0:T(1,128)S(1)} %bitcast.1, bf16[4,128,1024]{2,1,0:T(8,128)(2,1)S(1)} %copy-done, bf16[128,1024]{1,0:T(8,128)(2,1)S(1)} %copy-done.2, ...), custom_call_target="tpu_custom_call" | custom-call | tf_op jit(solution)/shard_map/pallas_call | solution.py:322
  38.8 0.7 %reshape.46 = f32[4,512]{1,0:T(4,128)} reshape(f32[4,8,64]{2,1,0:T(8,128)S(1)} %get-tuple-element.5) | data formatting | bytes 16384 | tf_op jit(solution)/shard_map/reshape | solution.py:356
  39.5 0.6 %copy.8 = f32[4,8,512]{2,1,0:T(8,128)} copy(f32[4,8,512]{2,1,0:T(8,128)S(1)} %get-tuple-element.14) | data formatting | bytes 131072
  (9 shorter events, 0.1 us)
Async XLA Ops:
  0.6 0.7 %copy-start.3 = (s32[4,64]{1,0:T(4,128)S(1)}, s32[4,64]{1,0:T(4,128)}, u32[]{:S(2)}) copy-start(s32[4,64]{1,0:T(4,128)} %param.9) | copy-start | bytes 3076
  1.3 0.7 %copy-start.4 = (s32[4,16]{1,0:T(4,128)S(1)}, s32[4,16]{1,0:T(4,128)}, u32[]{:S(2)}) copy-start(s32[4,16]{1,0:T(4,128)} %param.8) | copy-start | bytes 772
  3.0 1.2 %copy-start = (bf16[4,128,1024]{2,1,0:T(8,128)(2,1)S(1)}, bf16[4,128,1024]{2,1,0:T(8,128)(2,1)}, u32[]{:S(2)}) copy-start(bf16[4,128,1024]{2,1,0:T(8,128)(2,1)} %query_hbm.1) | copy-start | bytes 3145732
  4.2 1.2 %copy-start.1 = (bf16[512,1024]{1,0:T(8,128)(2,1)S(1)}, bf16[512,1024]{1,0:T(8,128)(2,1)}, u32[]{:S(2)}) copy-start(bf16[512,1024]{1,0:T(8,128)(2,1)} %fine_hbm.1) | copy-start | bytes 3145732
  5.5 0.9 %copy-start.2 = (bf16[128,1024]{1,0:T(8,128)(2,1)S(1)}, bf16[128,1024]{1,0:T(8,128)(2,1)}, u32[]{:S(2)}) copy-start(bf16[128,1024]{1,0:T(8,128)(2,1)} %coarse_hbm.1) | copy-start | bytes 786436

commit v3 on v2

--- a/solution.py
+++ b/solution.py
@@ -17,25 +17,17 @@
 MESH = pl.DeviceIdType.MESH
 
 
-def pack_requests(owners, local_ids, ncols, capacity):
-    count = owners.shape[0]
-    order = jnp.arange(count, dtype=jnp.int32)
-    earlier = (owners[:, None] == owners[None, :]) & (order[None, :] < order[:, None])
-    slots = jnp.sum(earlier.astype(jnp.int32), axis=1)
-    places = owners * capacity + slots
-    cells = jnp.arange(ncols * capacity, dtype=jnp.int32)
-    matches = places[:, None] == cells[None, :]
-    outgoing = jnp.sum(jnp.where(matches, local_ids[:, None] + 1, 0), axis=0) - 1
-    return (outgoing.reshape(ncols, capacity), places)
+def log2(value):
+    assert value & (value - 1) == 0
+    return value.bit_length() - 1
 
 
 def kernel(
     nrows,
     ncols,
     capacity,
-    request_ref,
-    place_ref,
-    parent_ref,
+    super_hbm,
+    pick_hbm,
     query_hbm,
     coarse_hbm,
     fine_hbm,
@@ -51,6 +43,11 @@
     near,
     far,
     weights,
+    chosen_ids,
+    picked_ids,
+    table,
+    request,
+    sorter,
     local_sem,
     across_sem,
     coarse_send,
@@ -75,6 +72,10 @@
     span = fine.shape[0]
     scale = math.log2(math.e) / math.sqrt(D)
 
+    super_copy = pltpu.make_async_copy(super_hbm, chosen_ids, local_sem.at[3])
+    pick_copy = pltpu.make_async_copy(pick_hbm, picked_ids, local_sem.at[4])
+    super_copy.start()
+    pick_copy.start()
     fine_copy = pltpu.make_async_copy(fine_hbm, fine, local_sem.at[0])
     query_copy = pltpu.make_async_copy(query_hbm, query, local_sem.at[1])
     own_copy = pltpu.make_async_copy(coarse_hbm, coarse.at[row], local_sem.at[2])
@@ -105,12 +106,49 @@
         team,
         lambda k: pl.semaphore_signal(barrier, inc=1, device_id=ahead(k), device_id_type=MESH),
     )
+
+    super_copy.wait()
+    pick_copy.wait()
+    ids = chosen_ids[...]
+    picks = picked_ids[...]
+    candidate = picks >> log2(SBLK)
+    parents = jnp.zeros_like(picks)
+    for i in range(ids.shape[1]):
+        parents = jnp.where(candidate == i, ids[:, i : i + 1], parents)
+    fine_ids = (parents << log2(SBLK)) + (picks & (SBLK - 1))
+    table[...] = jnp.zeros_like(table)
+    table[:blocks, :PICK] = ((fine_ids >> log2(span)) - base + ncols) & (ncols - 1)
+    table[blocks : 2 * blocks, :PICK] = fine_ids & (span - 1)
+    turned = jnp.transpose(table[...])
+    owners = jnp.concatenate([turned[:PICK, b : b + 1] for b in range(blocks)], axis=0)
+    local_ids = jnp.concatenate(
+        [turned[:PICK, blocks + b : blocks + b + 1] for b in range(blocks)], axis=0
+    )
+    count = blocks * PICK
+    marks = (owners == lax.broadcasted_iota(jnp.int32, (count, LANES), 1)).astype(jnp.float32)
+    earlier = lax.broadcasted_iota(jnp.int32, (count, count), 1) < lax.broadcasted_iota(
+        jnp.int32, (count, count), 0
+    )
+    ranks = jnp.dot(
+        earlier.astype(jnp.float32).astype(jnp.bfloat16),
+        marks.astype(jnp.bfloat16),
+        preferred_element_type=jnp.float32,
+    )
+    slots = jnp.sum(ranks * marks, axis=1, keepdims=True).astype(jnp.int32)
+    places = (owners & (half - 1)) * (2 * capacity) + (owners >> log2(half)) * capacity + slots
+    matches = places == lax.broadcasted_iota(jnp.int32, (count, ncols * capacity), 1)
+    sorter[...] = matches.astype(jnp.float32).astype(jnp.bfloat16)
+    outgoing = jnp.sum(jnp.where(matches, local_ids + 1, 0), axis=0, keepdims=True) - 1
+    for c in range(half):
+        request[c] = jnp.broadcast_to(
+            outgoing[:, c * 2 * capacity : (c + 1) * 2 * capacity], (8, 2 * capacity)
+        )
     pl.semaphore_wait(barrier, team)
 
     def ask_copy(k):
         target = ahead(k)
         return pltpu.make_async_remote_copy(
-            src_ref=request_ref.at[target[1] - base],
+            src_ref=request.at[target[1] - base],
             dst_ref=asked.at[k],
             send_sem=ask_send.at[k],
             recv_sem=ask_recv.at[k],
@@ -161,7 +199,7 @@
     across_copy.start()
     each(1, nrows, lambda k: coarse_copy(k).start())
 
-    asked[0] = request_ref[local]
+    asked[0] = request[local]
     row_iota = lax.broadcasted_iota(jnp.int32, (capacity, span), 1)
     fine_copy.wait()
     each(1, team, lambda k: ask_copy(k).wait_recv())
@@ -216,7 +254,7 @@
     own_copy.wait()
     each(1, nrows, lambda k: coarse_copy(k).wait_recv())
 
-    super_iota = lax.broadcasted_iota(jnp.int32, (supers, LANES), 0)
+    super_iota = lax.broadcasted_iota(jnp.int32, (supers, PICK), 0)
 
     def coarse_block(b, carry):
         for h in range(H):
@@ -231,39 +269,25 @@
             portion_ref[b, h : h + 1, :] = jnp.sum(raised * share, axis=0, keepdims=True) * (
                 supers / qtok
             )
-        chosen = (parent_ref[b] == super_iota).astype(jnp.float32)
+        return carry
+
+    lax.fori_loop(0, blocks, coarse_block, 0)
+    for b in range(blocks):
         weights[b] = jnp.dot(
             portion_ref[b],
-            chosen,
+            (parents[b : b + 1] == super_iota).astype(jnp.float32),
             preferred_element_type=jnp.float32,
             precision=lax.Precision.HIGHEST,
         )
-        return carry
-
-    lax.fori_loop(0, blocks, coarse_block, 0)
-
-    places = jnp.transpose(place_ref[...])
-    cell_iota = lax.broadcasted_iota(jnp.int32, (PICK, ncols * capacity), 1)
-    sorter = jnp.concatenate(
-        [
-            (places[:PICK, b : b + 1] == cell_iota).astype(jnp.float32).astype(jnp.bfloat16)
-            for b in range(blocks)
-        ],
-        axis=0,
-    )
-    cells = half * capacity
+
+    cells = ncols * capacity
     each(1, half, lambda k: near_copy(k).wait_recv())
     each(1, team, lambda k: far_copy(k).wait_recv())
     sums = [[] for _ in range(blocks)]
     for q in range(nrows):
+        joined = jnp.concatenate([near[:, :, q * part : (q + 1) * part], far[q]], axis=1)
         rows = jnp.dot(
-            sorter[:, :cells],
-            near[:, :, q * part : (q + 1) * part].reshape(cells, part),
-            preferred_element_type=jnp.float32,
-        ) + jnp.dot(
-            sorter[:, cells:],
-            far[q].reshape(cells, part),
-            preferred_element_type=jnp.float32,
+            sorter[...], joined.reshape(cells, part), preferred_element_type=jnp.float32
         )
         rows = rows.astype(jnp.bfloat16)
         for b in range(blocks):
@@ -280,8 +304,9 @@
                 share = 1.0 / jnp.sum(raised, axis=1, keepdims=True)
                 sums[b].append(jnp.sum(raised * share, axis=0, keepdims=True))
     for b in range(blocks):
-        selected_ref[b] = (
-            jnp.concatenate(sums[b], axis=0) * weights[b, :, :PICK] * (PICK / qtok)
+        final = jnp.concatenate(sums[b], axis=0) * weights[b] * (PICK / qtok)
+        selected_ref[b : b + 1, :] = jnp.concatenate(
+            [final[h : h + 1] for h in range(H)], axis=1
         )
 
     across_copy.wait_send()
@@ -302,30 +327,16 @@
     span = fine_keys.shape[0]
     part = width // nrows
     capacity = blocks // 4 * PICK
-    candidate = picks // SBLK
-    which = jnp.arange(super_ids.shape[1], dtype=jnp.int32)
-    parents = jnp.sum(
-        jnp.where(candidate[:, :, None] == which, super_ids[:, None, :], 0), axis=2
-    )
-    fine_ids = parents * SBLK + picks % SBLK
-    base = lax.axis_index("col") // half * half
-    owners = ((fine_ids // span - base + ncols) % ncols).reshape(-1)
-    local_ids = (fine_ids % span).reshape(-1)
-    outgoing, places = pack_requests(owners, local_ids, ncols, capacity)
-    outgoing = jnp.concatenate([outgoing[:half], outgoing[half:]], axis=1)
-    requests = jnp.broadcast_to(outgoing[:, None, :], (half, 8, 2 * capacity))
-    placed = jnp.pad(places.reshape(blocks, PICK), ((0, 8 - blocks), (0, LANES - PICK)))
-    parented = jnp.pad(parents, ((0, 0), (0, LANES - PICK)))[:, None, :]
     vmem = pl.BlockSpec(memory_space=pltpu.VMEM)
-    anywhere = pl.BlockSpec(memory_space=pl.ANY)
+    hbm = pl.BlockSpec(memory_space=pltpu.HBM)
     dma = pltpu.SemaphoreType.DMA
     portion, selected = pl.pallas_call(
         functools.partial(kernel, nrows, ncols, capacity),
         out_shape=(
             jax.ShapeDtypeStruct((blocks, H, supers), jnp.float32),
-            jax.ShapeDtypeStruct((blocks, H, PICK), jnp.float32),
+            jax.ShapeDtypeStruct((blocks, H * PICK), jnp.float32),
         ),
-        in_specs=[vmem] * 3 + [anywhere] * 3,
+        in_specs=[hbm] * 5,
         out_specs=(vmem, vmem),
         scratch_shapes=[
             pltpu.VMEM((blocks, qtok, width), jnp.bfloat16),
@@ -337,8 +348,13 @@
             pltpu.VMEM((team, capacity, part), jnp.bfloat16),
             pltpu.VMEM((half, capacity, width), jnp.bfloat16),
             pltpu.VMEM((nrows, half, capacity, part), jnp.bfloat16),
-            pltpu.VMEM((blocks, H, LANES), jnp.float32),
-            dma((3,)),
+            pltpu.VMEM((blocks, H, PICK), jnp.float32),
+            pltpu.VMEM(super_ids.shape, jnp.int32),
+            pltpu.VMEM(picks.shape, jnp.int32),
+            pltpu.VMEM((2 * blocks, LANES), jnp.int32),
+            pltpu.VMEM((half, 8, 2 * capacity), jnp.int32),
+            pltpu.VMEM((blocks * PICK, ncols * capacity), jnp.bfloat16),
+            dma((5,)),
             dma((2,)),
             dma((nrows,)),
             dma((nrows,)),
@@ -350,10 +366,10 @@
             dma((team,)),
         ],
         compiler_params=pltpu.CompilerParams(
-            collective_id=0, has_side_effects=True, vmem_limit_bytes=50 * 1024 * 1024
+            collective_id=0, has_side_effects=True, vmem_limit_bytes=63963136
         ),
-    )(requests, placed, parented, queries, coarse_keys, fine_keys)
-    return (portion, selected.reshape(blocks, H * PICK))
+    )(super_ids, picks, queries, coarse_keys, fine_keys)
+    return (portion, selected)
 
 
 def solution(mesh):

time: 40.4 us -> 35.4 us (0.88)
  local copies, waits for them, and re-layouts: 6.47 us -> 2.08 us
  other arithmetic: 0.56 us -> 0 us
    unnamed x11 -> x4, local copies, waits for them, and re-layouts: 5.37 us -> 2.08 us
    reshape x2 -> x0, local copies, waits for them, and re-layouts: 0.76 us -> none  [the longest x1 0.68 us: per_device(): return (portion, selected.reshape(blocks, H * PICK))]
    reduce_sum x3 -> x0, other arithmetic: 0.42 us -> none  [the longest x1 0.18 us: pack_requests(): slots = jnp.sum(earlier.astype(jnp.int32), axis=1)]
where the time goes in v3:
time: 35.4 us; the launch traced here: 35.3 us
  Pallas kernels  32.5 us (92%)
  local copies, waits for them, and re-layouts  2.08 us (6%)
  between operations  0.65 us (2%)
    pallas_call x1, Pallas kernels, per_device(): pl.pallas_call(functools.partial(kernel, nrows, ncols, capacity), out_sha...  32.5 us
    unnamed x4, local copies, waits for them, and re-layouts  2.08 us

profile of v3, /device:TPU:0, one launch (start us, length us, event | category | flops | bytes accessed | tf_op | source)
XLA Modules:
  0.0 35.3 jit_solution(9774772638663121031)
XLA Ops:
  0.6 32.5 %shard_map.68 = (f32[4,8,512]{2,1,0:T(8,128)}, f32[4,512]{1,0:T(4,128)}) custom-call(s32[4,16]{1,0:T(4,128)} %super_hbm.1, s32[4,64]{1,0:T(4,128)} %pick_hbm.1, bf16[4,128,1024]{2,1,0:T(8,128)(2,1)} %query_hbm.1, bf16[128,1024]{1,0:T(8,128)(2,1)} %coarse_hbm.1, bf16[512,1024]{1,0:T(8,128)(2,1)} %fine_hbm.1), custom_call_target="tpu_custom_call" | custom-call | tf_op jit(solution)/shard_map/pallas_call | solution.py:333
  33.2 0.0 copy-start
  33.2 1.5 %copy.9 = f32[4,8,512]{2,1,0:T(8,128)} copy(f32[4,8,512]{2,1,0:T(8,128)} %get-tuple-element.4) | data formatting | bytes 131072
  34.7 0.0 copy-done
  34.7 0.6 %copy.10 = f32[4,512]{1,0:T(4,128)} copy(f32[4,512]{1,0:T(4,128)S(1)} %copy-done) | data formatting | bytes 16384
Async XLA Ops:
  33.2 1.5 %copy-start = (f32[4,512]{1,0:T(4,128)S(1)}, f32[4,512]{1,0:T(4,128)}, u32[]{:S(2)}) copy-start(f32[4,512]{1,0:T(4,128)} %get-tuple-element.5) | copy-start | bytes 24580

commit v4 on v3

--- a/solution.py
+++ b/solution.py
@@ -68,6 +68,7 @@
     me = row * half + local
     blocks, qtok, width = query.shape
     part = width // nrows
+    pieces = part // D
     supers = nrows * coarse.shape[1]
     span = fine.shape[0]
     scale = math.log2(math.e) / math.sqrt(D)
@@ -156,14 +157,15 @@
             device_id_type=MESH,
         )
 
-    across_copy = pltpu.make_async_remote_copy(
-        src_ref=fine_hbm.at[:, pl.ds(pl.multiple_of(row * part, part), part)],
-        dst_ref=across,
-        send_sem=across_sem.at[0],
-        recv_sem=across_sem.at[1],
-        device_id=opposite,
-        device_id_type=MESH,
-    )
+    def across_copy(i):
+        return pltpu.make_async_remote_copy(
+            src_ref=fine_hbm.at[:, pl.ds(pl.multiple_of(row * part + i * D, D), D)],
+            dst_ref=across.at[i],
+            send_sem=across_sem.at[i],
+            recv_sem=across_sem.at[pieces + i],
+            device_id=opposite,
+            device_id_type=MESH,
+        )
 
     def near_copy(k):
         return pltpu.make_async_remote_copy(
@@ -175,12 +177,12 @@
             device_id_type=MESH,
         )
 
-    def far_copy(k):
-        return pltpu.make_async_remote_copy(
-            src_ref=far_staged.at[k],
-            dst_ref=far.at[row, local],
-            send_sem=far_send.at[k],
-            recv_sem=far_recv.at[k],
+    def far_copy(p, k):
+        return pltpu.make_async_remote_copy(
+            src_ref=far_staged.at[p, k],
+            dst_ref=far.at[row, p, local],
+            send_sem=far_send.at[p, k],
+            recv_sem=far_recv.at[p, k],
             device_id=behind(k),
             device_id_type=MESH,
         )
@@ -196,7 +198,7 @@
         )
 
     each(1, team, lambda k: ask_copy(k).start())
-    across_copy.start()
+    each(0, pieces, lambda i: across_copy(i).start())
     each(1, nrows, lambda k: coarse_copy(k).start())
 
     asked[0] = request[local]
@@ -229,26 +231,26 @@
 
     lax.fori_loop(0, half // GROUP, near_group, 0)
     near[local] = near_staged[0]
-    across_copy.wait_recv()
-
-    def far_group(g, carry):
+    def far_group(p, g, carry):
         picked = [one_hot(g * GROUP + i, capacity) for i in range(GROUP)]
         found = jnp.dot(
-            jnp.concatenate(picked, axis=0), across[...], preferred_element_type=jnp.float32
+            jnp.concatenate(picked, axis=0), across[p], preferred_element_type=jnp.float32
         ).astype(jnp.bfloat16)
         for i in range(GROUP):
-            far_staged[g * GROUP + i] = found[i * capacity : (i + 1) * capacity]
+            far_staged[p, g * GROUP + i] = found[i * capacity : (i + 1) * capacity]
         for i in range(GROUP):
             k = g * GROUP + i
 
             @pl.when(k > 0)
             def _():
-                far_copy(k).start()
+                far_copy(p, k).start()
 
         return carry
 
-    lax.fori_loop(0, team // GROUP, far_group, 0)
-    far[row, local] = far_staged[0]
+    for p in range(pieces):
+        across_copy(p).wait_recv()
+        lax.fori_loop(0, team // GROUP, functools.partial(far_group, p), 0)
+        far[row, p, local] = far_staged[p, 0]
 
     query_copy.wait()
     own_copy.wait()
@@ -282,10 +284,12 @@
 
     cells = ncols * capacity
     each(1, half, lambda k: near_copy(k).wait_recv())
-    each(1, team, lambda k: far_copy(k).wait_recv())
+    for p in range(pieces):
+        each(1, team, lambda k: far_copy(p, k).wait_recv())
     sums = [[] for _ in range(blocks)]
     for q in range(nrows):
-        joined = jnp.concatenate([near[:, :, q * part : (q + 1) * part], far[q]], axis=1)
+        remote = jnp.concatenate([far[q, p] for p in range(pieces)], axis=2)
+        joined = jnp.concatenate([near[:, :, q * part : (q + 1) * part], remote], axis=1)
         rows = jnp.dot(
             sorter[...], joined.reshape(cells, part), preferred_element_type=jnp.float32
         )
@@ -309,10 +313,11 @@
             [final[h : h + 1] for h in range(H)], axis=1
         )
 
-    across_copy.wait_send()
+    each(0, pieces, lambda i: across_copy(i).wait_send())
     each(1, team, lambda k: ask_copy(k).wait_send())
     each(1, half, lambda k: near_copy(k).wait_send())
-    each(1, team, lambda k: far_copy(k).wait_send())
+    for p in range(pieces):
+        each(1, team, lambda k: far_copy(p, k).wait_send())
     each(1, nrows, lambda k: coarse_copy(k).wait_send())
 
 
@@ -326,6 +331,7 @@
     supers = shard * nrows
     span = fine_keys.shape[0]
     part = width // nrows
+    pieces = part // D
     capacity = blocks // 4 * PICK
     vmem = pl.BlockSpec(memory_space=pltpu.VMEM)
     hbm = pl.BlockSpec(memory_space=pltpu.HBM)
@@ -342,12 +348,12 @@
             pltpu.VMEM((blocks, qtok, width), jnp.bfloat16),
             pltpu.VMEM((span, width), jnp.bfloat16),
             pltpu.VMEM((nrows, shard, width), jnp.bfloat16),
-            pltpu.VMEM((span, part), jnp.bfloat16),
+            pltpu.VMEM((pieces, span, D), jnp.bfloat16),
             pltpu.VMEM((team, 8, 2 * capacity), jnp.int32),
             pltpu.VMEM((half, capacity, width), jnp.bfloat16),
-            pltpu.VMEM((team, capacity, part), jnp.bfloat16),
+            pltpu.VMEM((pieces, team, capacity, D), jnp.bfloat16),
             pltpu.VMEM((half, capacity, width), jnp.bfloat16),
-            pltpu.VMEM((nrows, half, capacity, part), jnp.bfloat16),
+            pltpu.VMEM((nrows, pieces, half, capacity, D), jnp.bfloat16),
             pltpu.VMEM((blocks, H, PICK), jnp.float32),
             pltpu.VMEM(super_ids.shape, jnp.int32),
             pltpu.VMEM(picks.shape, jnp.int32),
@@ -355,15 +361,15 @@
             pltpu.VMEM((half, 8, 2 * capacity), jnp.int32),
             pltpu.VMEM((blocks * PICK, ncols * capacity), jnp.bfloat16),
             dma((5,)),
-            dma((2,)),
+            dma((2 * pieces,)),
             dma((nrows,)),
             dma((nrows,)),
             dma((team,)),
             dma((team,)),
             dma((half,)),
             dma((half,)),
-            dma((team,)),
-            dma((team,)),
+            dma((pieces, team)),
+            dma((pieces, team)),
         ],
         compiler_params=pltpu.CompilerParams(
             collective_id=0, has_side_effects=True, vmem_limit_bytes=63963136

time: 35.4 us -> 34.8 us (0.983)
  Pallas kernels: 32.5 us -> 31.9 us
    pallas_call x1, Pallas kernels: 32.5 us -> 31.9 us  [per_device(): pl.pallas_call(functools.partial(kernel, nrows, ncols, capacity), out_sha...]
where the time goes in v4:
time: 34.8 us; the launch traced here: 34.7 us
  Pallas kernels  31.9 us (92%)
  local copies, waits for them, and re-layouts  2.08 us (6%)
  between operations  0.65 us (2%)
    pallas_call x1, Pallas kernels, per_device(): pl.pallas_call(functools.partial(kernel, nrows, ncols, capacity), out_sha...  31.9 us
    unnamed x4, local copies, waits for them, and re-layouts  2.08 us

profile of v4, /device:TPU:0, one launch (start us, length us, event | category | flops | bytes accessed | tf_op | source)
XLA Modules:
  0.0 34.7 jit_solution(7021754799915451909)
XLA Ops:
  0.6 31.9 %shard_map.68 = (f32[4,8,512]{2,1,0:T(8,128)}, f32[4,512]{1,0:T(4,128)}) custom-call(s32[4,16]{1,0:T(4,128)} %super_hbm.1, s32[4,64]{1,0:T(4,128)} %pick_hbm.1, bf16[4,128,1024]{2,1,0:T(8,128)(2,1)} %query_hbm.1, bf16[128,1024]{1,0:T(8,128)(2,1)} %coarse_hbm.1, bf16[512,1024]{1,0:T(8,128)(2,1)} %fine_hbm.1), custom_call_target="tpu_custom_call" | custom-call | tf_op jit(solution)/shard_map/pallas_call | solution.py:339
  32.6 0.0 copy-start
  32.6 1.5 %copy.9 = f32[4,8,512]{2,1,0:T(8,128)} copy(f32[4,8,512]{2,1,0:T(8,128)} %get-tuple-element.4) | data formatting | bytes 131072
  34.0 0.0 copy-done
  34.1 0.6 %copy.10 = f32[4,512]{1,0:T(4,128)} copy(f32[4,512]{1,0:T(4,128)S(1)} %copy-done) | data formatting | bytes 16384
Async XLA Ops:
  32.6 1.5 %copy-start = (f32[4,512]{1,0:T(4,128)S(1)}, f32[4,512]{1,0:T(4,128)}, u32[]{:S(2)}) copy-start(f32[4,512]{1,0:T(4,128)} %get-tuple-element.5) | copy-start | bytes 24580
